TPU v7x, 32 devices: a whole 2x2x4 slice. The times are simulated.
32 devices in a mesh: dp: 8 (over y, x, core), tensor: 4 (over z).
Axes of the slice: x: 2, y: 2, z: 4, core: 2. Of those that a mesh axis runs over, the one named last changes fastest.
Arguments:
- layer_input: bfloat16 [12288, 2048], P('dp'), may hold values from -30 to 30
- cotangent: bfloat16 [12288, 2048], P('dp'), may hold values from -6 to 6
- lengths: int32 [24], P('dp'), may hold values from 0 to 512, as said below
- projector: float32 [2048, 6144], P('dp', 'tensor'), may hold values from -0.125 to 0.125
- projector_moments: float32 [2, 2048, 6144], P(None, 'dp', 'tensor'), as said below
- shifts: float32 [8, 768], P('tensor', 'dp'), may hold values from -3 to 3
- shifts_moments: float32 [2, 8, 768], P(None, 'tensor', 'dp'), as said below
- combiner: float32 [2048, 2048], P('tensor', 'dp'), may hold values from -1.5 to 1.5
- combiner_moments: float32 [2, 2048, 2048], P(None, 'tensor', 'dp'), as said below
- expander: float32 [2048, 8192], P('dp', 'tensor'), may hold values from -0.125 to 0.125
- expander_moments: float32 [2, 2048, 8192], P(None, 'dp', 'tensor'), as said below
- offsets: float32 [8, 1024], P('tensor', 'dp'), may hold values from -3 to 3
- offsets_moments: float32 [2, 8, 1024], P(None, 'tensor', 'dp'), as said below
- reducer: float32 [8192, 2048], P('tensor', 'dp'), may hold values from -0.0625 to 0.0625
- reducer_moments: float32 [2, 8192, 2048], P(None, 'tensor', 'dp'), as said below
- vectors: float32 [6, 2048], P(None, ('dp', 'tensor')), may hold values from -2 to 2
- vectors_moments: float32 [2, 6, 2048], P(None, None, ('dp', 'tensor')), as said below
Outputs:
- layer_output: bfloat16 [12288, 2048], P('dp', 'tensor')
- input_gradient: bfloat16 [12288, 2048], P('dp', 'tensor')
- projector_gradient: float32 [2048, 6144], P('dp', 'tensor')
- projector_states: float32 [2, 2048, 6144], P(None, 'dp', 'tensor')
- projector_update: float32 [2048, 6144], P('dp', 'tensor')
- shifts_gradient: float32 [8, 768], P('tensor', 'dp')
- shifts_states: float32 [2, 8, 768], P(None, 'tensor', 'dp')
- shifts_update: float32 [8, 768], P('tensor', 'dp')
- combiner_gradient: float32 [2048, 2048], P('tensor', 'dp')
- combiner_states: float32 [2, 2048, 2048], P(None, 'tensor', 'dp')
- combiner_update: float32 [2048, 2048], P('tensor', 'dp')
- expander_gradient: float32 [2048, 8192], P('dp', 'tensor')
- expander_states: float32 [2, 2048, 8192], P(None, 'dp', 'tensor')
- expander_update: float32 [2048, 8192], P('dp', 'tensor')
- offsets_gradient: float32 [8, 1024], P('tensor', 'dp')
- offsets_states: float32 [2, 8, 1024], P(None, 'tensor', 'dp')
- offsets_update: float32 [8, 1024], P('tensor', 'dp')
- reducer_gradient: float32 [8192, 2048], P('tensor', 'dp')
- reducer_states: float32 [2, 8192, 2048], P(None, 'tensor', 'dp')
- reducer_update: float32 [8192, 2048], P('tensor', 'dp')
- vectors_gradient: float32 [6, 2048], P(None, ('dp', 'tensor'))
- vectors_states: float32 [2, 6, 2048], P(None, None, ('dp', 'tensor'))
- vectors_update: float32 [6, 2048], P(None, ('dp', 'tensor'))
Inputs may be any that keep to these rules, and one draw needn't show every extreme that they name: `lengths`: dp index i holds slots i * 3 to i * 3 + 2; a slot is empty (0) or holds one sequence of 128 to 512 tokens; every index holds at least one sequence, some index has all its slots filled, one of them with 512 tokens, and some index holds exactly one sequence. `projector_moments`: the roots of the second moments (index 1 of the first dimension) are positive. `shifts_moments`: the roots of the second moments are positive. `combiner_moments`: the roots of the second moments are positive. `expander_moments`: the roots of the second moments are positive. `offsets_moments`: the roots of the second moments are positive. `reducer_moments`: the roots of the second moments are positive. `vectors_moments`: the roots of the second moments are positive.
All inputs are finite; a program needn't handle non-finite values.
Results may differ from a plain program's by a relative error of at most 0.014.
The roundings to bfloat16 on the way count: a program that leaves them out, or rounds other values in their place, can miss the bound.
Values may be sent and summed in bfloat16 or wider, within the bound.
A program may use at most 320 MiB of HBM per device.

v0:
```python
import math
import jax
import jax.numpy as jnp
from jax import lax
from jax.sharding import PartitionSpec as P

HD = 256
ROT = 64
SEQ_LEN = 512
STEP = 10
layer_eps = 1e-05
adam_eps = 1e-08
beta_one = 0.9
beta_two = 0.95
learn_rate = 0.02
decay_rate = 0.01
rotary_base = 10000.0


def norm_layer(values, scale_row, shift_row):
    average = jnp.mean(values, axis=-1, keepdims=True)
    centred = values - average
    variance = jnp.mean(centred * centred, axis=-1, keepdims=True)
    return centred * lax.rsqrt(variance + layer_eps) * scale_row + shift_row


def exact_gelu(values):
    return jax.nn.gelu(values, approximate=False)


def rotary_tables():
    half_rot = ROT // 2
    frequency = jnp.exp(
        jnp.arange(half_rot, dtype=jnp.float32) * (-2.0 * math.log(rotary_base) / ROT)
    )
    angles = jnp.arange(SEQ_LEN, dtype=jnp.float32)[:, None] * frequency[None, :]
    return (jnp.cos(angles)[:, None, :], jnp.sin(angles)[:, None, :])


def rotate(values, cos_table, sin_table):
    half_rot = ROT // 2
    leading = values[..., :half_rot]
    trailing = values[..., half_rot:ROT]
    return jnp.concatenate(
        [
            leading * cos_table - trailing * sin_table,
            trailing * cos_table + leading * sin_table,
            values[..., ROT:],
        ],
        axis=-1,
    )


def allowed_mask(length):
    position = jnp.arange(SEQ_LEN)
    return (position[None, :] <= position[:, None]) & (position[None, :] < jnp.maximum(length, 1))


def contract_rows(left, right):
    return lax.dot_general(
        left, right, (((0,), (0,)), ((), ())), preferred_element_type=jnp.float32
    )


def contract_cols(left, right):
    return lax.dot_general(
        left, right, (((1,), (1,)), ((), ())), preferred_element_type=jnp.float32
    )


def masked_scores(query_rows, key_rows, length):
    scores = jnp.einsum(
        "qhd,khd->hqk", query_rows, key_rows, preferred_element_type=jnp.float32
    ) * HD ** (-0.5)
    return jnp.where(allowed_mask(length)[None], scores, -1e30)


def attend_forward(query_rows, key_rows, value_rows, length):
    scores = masked_scores(query_rows, key_rows, length)
    largest = jnp.max(scores, axis=-1, keepdims=True)
    powers = jnp.exp(scores - largest)
    row_total = jnp.sum(powers, axis=-1, keepdims=True)
    weights = (powers / row_total).astype(jnp.bfloat16)
    mixture = jnp.einsum("hqk,khd->qhd", weights, value_rows, preferred_element_type=jnp.float32)
    return (mixture.astype(jnp.bfloat16), (largest + jnp.log(row_total))[..., 0])


def attend_backward(query_rows, key_rows, value_rows, length, summary, incoming):
    scores = masked_scores(query_rows, key_rows, length)
    weights = jnp.exp(scores - summary[..., None])
    pushed = jnp.einsum("qhd,khd->hqk", incoming, value_rows, preferred_element_type=jnp.float32)
    inner_sum = jnp.sum(weights * pushed, axis=-1, keepdims=True)
    dscores = (weights * (pushed - inner_sum)).astype(jnp.bfloat16)
    score_scale = HD ** (-0.5)
    grad_query = (
        jnp.einsum("hqk,khd->qhd", dscores, key_rows, preferred_element_type=jnp.float32)
        * score_scale
    )
    grad_keys = (
        jnp.einsum("hqk,qhd->khd", dscores, query_rows, preferred_element_type=jnp.float32)
        * score_scale
    )
    grad_values = jnp.einsum(
        "hqk,qhd->khd", weights.astype(jnp.bfloat16), incoming, preferred_element_type=jnp.float32
    )
    return (grad_query, grad_keys, grad_values)


def forward_slot(pieces):
    query_rows, key_rows, value_rows, length = pieces
    return attend_forward(query_rows, key_rows, value_rows, length)


def backward_slot(pieces):
    query_rows, key_rows, value_rows, length, summary, incoming = pieces
    return attend_backward(query_rows, key_rows, value_rows, length, summary, incoming)


def adamw(master, moments, gradient):
    first_moment = beta_one * moments[0] + (1.0 - beta_one) * gradient
    root_moment = jnp.sqrt(
        beta_two * moments[1] * moments[1] + (1.0 - beta_two) * gradient * gradient
    )
    first_hat = first_moment / (1.0 - beta_one**STEP)
    root_hat = root_moment / math.sqrt(1.0 - beta_two**STEP)
    update = -learn_rate * (first_hat / (root_hat + adam_eps) + decay_rate * master)
    return (jnp.stack([first_moment, root_moment]), update)


def on_device(
    layer_input,
    cotangent,
    lengths,
    projector,
    projector_moments,
    shifts,
    shifts_moments,
    combiner,
    combiner_moments,
    expander,
    expander_moments,
    offsets,
    offsets_moments,
    reducer,
    reducer_moments,
    vectors,
    vectors_moments,
):
    entry, entry_shift, combine, expand, expand_shift, shrink = (
        lax.all_gather(projector.astype(jnp.bfloat16), "dp", axis=0, tiled=True),
        lax.all_gather(shifts.astype(jnp.bfloat16), "dp", axis=1, tiled=True),
        lax.all_gather(combiner.astype(jnp.bfloat16), "dp", axis=1, tiled=True),
        lax.all_gather(expander.astype(jnp.bfloat16), "dp", axis=0, tiled=True),
        lax.all_gather(offsets.astype(jnp.bfloat16), "dp", axis=1, tiled=True),
        lax.all_gather(reducer.astype(jnp.bfloat16), "dp", axis=1, tiled=True),
    )
    full_vectors = lax.all_gather(
        vectors.astype(jnp.bfloat16), ("dp", "tensor"), axis=1, tiled=True
    ).astype(jnp.float32)
    slot_count = lengths.shape[0]
    row_count = slot_count * SEQ_LEN
    local_heads = entry.shape[1] // (3 * HD)
    cos_table, sin_table = rotary_tables()
    inputs = layer_input.astype(jnp.float32)
    first_norm, first_back = jax.vjp(norm_layer, inputs, full_vectors[0], full_vectors[1])
    normed_one = first_norm.astype(jnp.bfloat16)
    packed = jnp.dot(normed_one, entry, preferred_element_type=jnp.float32) + entry_shift.astype(
        jnp.float32
    ).reshape(-1)
    packed = packed.reshape(slot_count, SEQ_LEN, local_heads, 3, HD)
    query_rows = rotate(packed[:, :, :, 0], cos_table, sin_table).astype(jnp.bfloat16)
    key_rows = rotate(packed[:, :, :, 1], cos_table, sin_table).astype(jnp.bfloat16)
    value_rows = packed[:, :, :, 2].astype(jnp.bfloat16)
    mixture, summary = lax.map(forward_slot, (query_rows, key_rows, value_rows, lengths))
    attended = mixture.reshape(row_count, local_heads * HD)
    second_norm, second_back = jax.vjp(norm_layer, inputs, full_vectors[2], full_vectors[3])
    normed_two = second_norm.astype(jnp.bfloat16)
    hidden = jnp.dot(normed_two, expand, preferred_element_type=jnp.float32) + expand_shift.astype(
        jnp.float32
    ).reshape(-1)
    activated, gelu_back = jax.vjp(exact_gelu, hidden)
    activated = activated.astype(jnp.bfloat16)
    partial_sum = jnp.dot(attended, combine, preferred_element_type=jnp.float32) + jnp.dot(
        activated, shrink, preferred_element_type=jnp.float32
    )
    summed = lax.psum_scatter(
        partial_sum.astype(jnp.bfloat16), "tensor", scatter_dimension=1, tiled=True
    ).astype(jnp.float32)
    own_width = summed.shape[1]
    own_start = lax.axis_index("tensor") * own_width
    own_input = lax.dynamic_slice_in_dim(inputs, own_start, own_width, 1)
    own_bias = lax.dynamic_slice_in_dim(full_vectors[4] + full_vectors[5], own_start, own_width, 0)
    live_rows = (
        (jnp.arange(SEQ_LEN)[None, :] < lengths[:, None]).astype(jnp.float32).reshape(row_count, 1)
    )
    layer_output = (live_rows * (own_input + summed + own_bias)).astype(jnp.bfloat16)
    upstream_float = cotangent.astype(jnp.float32) * live_rows
    upstream = upstream_float.astype(jnp.bfloat16)
    dactivated = contract_cols(upstream, shrink)
    dhidden = gelu_back(dactivated)[0].astype(jnp.bfloat16)
    expand_local = contract_rows(normed_two, dhidden)
    expand_bias_local = jnp.sum(dhidden.astype(jnp.float32), axis=0).reshape(expand_shift.shape)
    shrink_local = contract_rows(activated, upstream)
    dnormed_two = contract_cols(dhidden, expand)
    dattended = contract_cols(upstream, combine).astype(jnp.bfloat16)
    combine_local = contract_rows(attended, upstream)
    incoming = dattended.reshape(slot_count, SEQ_LEN, local_heads, HD)
    grad_query, grad_keys, grad_values = lax.map(
        backward_slot, (query_rows, key_rows, value_rows, lengths, summary, incoming)
    )
    grad_query = rotate(grad_query, cos_table, -sin_table)
    grad_keys = rotate(grad_keys, cos_table, -sin_table)
    dpacked = (
        jnp.stack([grad_query, grad_keys, grad_values], axis=3)
        .reshape(row_count, 3 * local_heads * HD)
        .astype(jnp.bfloat16)
    )
    entry_local = contract_rows(normed_one, dpacked)
    entry_bias_local = jnp.sum(dpacked.astype(jnp.float32), axis=0).reshape(entry_shift.shape)
    dnormed_one = contract_cols(dpacked, entry)
    dinput_one, dscale_one, dshift_one = first_back(dnormed_one)
    dinput_two, dscale_two, dshift_two = second_back(dnormed_two)
    bias_total = jnp.sum(upstream_float, axis=0)
    vector_local = jnp.stack(
        [dscale_one, dshift_one, dscale_two, dshift_two, bias_total, bias_total]
    )
    (
        entry_share,
        entry_bias_share,
        combine_share,
        vector_share,
        expand_share,
        expand_bias_share,
        shrink_share,
    ) = (
        lax.psum_scatter(entry_local, "dp", scatter_dimension=0, tiled=True),
        lax.psum_scatter(entry_bias_local, "dp", scatter_dimension=1, tiled=True),
        lax.psum_scatter(combine_local, "dp", scatter_dimension=1, tiled=True),
        lax.psum_scatter(vector_local, "dp", scatter_dimension=1, tiled=True),
        lax.psum_scatter(expand_local, "dp", scatter_dimension=0, tiled=True),
        lax.psum_scatter(expand_bias_local, "dp", scatter_dimension=1, tiled=True),
        lax.psum_scatter(shrink_local, "dp", scatter_dimension=1, tiled=True),
    )
    input_part, norm_share = (
        lax.psum_scatter(
            (dinput_one + dinput_two).astype(jnp.bfloat16),
            "tensor",
            scatter_dimension=1,
            tiled=True,
        ).astype(jnp.float32),
        lax.psum_scatter(
            vector_share[:4].astype(jnp.bfloat16), "tensor", scatter_dimension=1, tiled=True
        ).astype(jnp.float32),
    )
    own_cot = lax.dynamic_slice_in_dim(upstream_float, own_start, own_width, 1)
    input_gradient = (input_part + own_cot).astype(jnp.bfloat16)
    piece_width = vector_share.shape[1] // lax.axis_size("tensor")
    bias_share = lax.dynamic_slice_in_dim(
        vector_share[4:], lax.axis_index("tensor") * piece_width, piece_width, 1
    )
    vector_gradient = jnp.concatenate([norm_share, bias_share], axis=0)
    projector_states, projector_update = adamw(projector, projector_moments, entry_share)
    shifts_states, shifts_update = adamw(shifts, shifts_moments, entry_bias_share)
    combiner_states, combiner_update = adamw(combiner, combiner_moments, combine_share)
    expander_states, expander_update = adamw(expander, expander_moments, expand_share)
    offsets_states, offsets_update = adamw(offsets, offsets_moments, expand_bias_share)
    reducer_states, reducer_update = adamw(reducer, reducer_moments, shrink_share)
    vectors_states, vectors_update = adamw(vectors, vectors_moments, vector_gradient)
    return (
        layer_output,
        input_gradient,
        entry_share,
        projector_states,
        projector_update,
        entry_bias_share,
        shifts_states,
        shifts_update,
        combine_share,
        combiner_states,
        combiner_update,
        expand_share,
        expander_states,
        expander_update,
        expand_bias_share,
        offsets_states,
        offsets_update,
        shrink_share,
        reducer_states,
        reducer_update,
        vector_gradient,
        vectors_states,
        vectors_update,
    )


def solution(mesh):
    placed = (
        P("dp", None),
        P("dp", None),
        P("dp"),
        P("dp", "tensor"),
        P(None, "dp", "tensor"),
        P("tensor", "dp"),
        P(None, "tensor", "dp"),
        P("tensor", "dp"),
        P(None, "tensor", "dp"),
        P("dp", "tensor"),
        P(None, "dp", "tensor"),
        P("tensor", "dp"),
        P(None, "tensor", "dp"),
        P("tensor", "dp"),
        P(None, "tensor", "dp"),
        P(None, ("dp", "tensor")),
        P(None, None, ("dp", "tensor")),
    )
    return jax.shard_map(
        on_device,
        mesh=mesh,
        in_specs=placed,
        out_specs=(
            P("dp", "tensor"),
            P("dp", "tensor"),
            P("dp", "tensor"),
            P(None, "dp", "tensor"),
            P("dp", "tensor"),
            P("tensor", "dp"),
            P(None, "tensor", "dp"),
            P("tensor", "dp"),
            P("tensor", "dp"),
            P(None, "tensor", "dp"),
            P("tensor", "dp"),
            P("dp", "tensor"),
            P(None, "dp", "tensor"),
            P("dp", "tensor"),
            P("tensor", "dp"),
            P(None, "tensor", "dp"),
            P("tensor", "dp"),
            P("tensor", "dp"),
            P(None, "tensor", "dp"),
            P("tensor", "dp"),
            P(None, ("dp", "tensor")),
            P(None, None, ("dp", "tensor")),
            P(None, ("dp", "tensor")),
        ),
        check_vma=False,
    )
```

profile of v0, /device:TPU:0, one launch (start us, length us, event | category | flops | bytes accessed | tf_op | source)
XLA Modules:
  0.0 1193.2 jit_solution(17004085662014109550)
XLA Ops:
  7.3 2.4 convert_element_type.123
  9.7 2.7 convert_element_type.128
  12.6 10.3 all-gather.1
  23.0 69.1 %all-gather = bf16[32,64,6]{1,2,0:T(8,128)(2,1)S(1)} all-gather(bf16[1,64,6]{1,2,0:T(8,128)(2,1)S(1)} %convert_bitcast_fusion.1), channel_id=1, replica_groups=mesh['dp'=8,'tensor'=4] {'dp','tensor'}, dimensions={0}, use_global_device_ids=true | all-gather | bytes 25344 | tf_op jit(solution)/shard_map/all_gather | solution.py:157
  92.2 9.1 all_gather.26
  101.3 3.7 convert_reduce_fusion.2
  105.0 4.6 multiply_reduce_fusion.5
  109.6 1.7 fusion.61
  112.2 16.0 %convolution_add_fusion = f32[1536,1536]{1,0:T(8,128)} fusion(bf16[2048,1536]{1,0:T(8,128)(2,1)} %all-gather.7.cloned.1.call-done, f32[1536]{0:T(1024)S(1)} %reshape.413, bf16[1536,2048]{1,0:T(8,128)(2,1)} %param.21, f32[2048]{0:T(1024)S(1)} %bitcast.340, f32[2048]{0:T(1024)S(1)} %bitcast.321, f32[1536]{0:T(1024)S(1)} %fusion.64, ...), kind=kOutput, calls=%fused_computation.89 | convolution fusion | flops 9684910080 | bytes 22054912 | tf_op jit(solution)/shard_map/dot_general | solution.py:167
  128.2 15.8 %reshape.403 = f32[3,512,2,3,256]{4,3,2,1,0:T(4,128)} reshape(f32[1536,1536]{1,0:T(8,128)} %convolution_add_fusion) | data formatting | bytes 18874368 | tf_op jit(solution)/shard_map/reshape | solution.py:170
  144.0 7.8 slice.258
  151.8 6.6 copy.186
  158.3 13.5 %fusion.105 = (f32[3,512,2,1,256]{4,3,2,1,0:T(1,128)S(1)}, f32[3,512,2,1,256]{4,3,2,1,0:T(1,128)S(1)}) fusion(f32[3,512,2,3,256]{4,3,2,1,0:T(4,128)} %reshape.403), kind=kLoop, calls=%fused_computation.225 | loop fusion | bytes 12582912 | tf_op jit(solution)/shard_map/slice | solution.py:172
  173.5 1.7 slice.257
  176.9 1.7 slice.256
  178.6 4.5 subtract_convert_fusion
  183.1 11.1 pad_maximum_fusion.3
  195.9 23.0 %while.26 = (s32[]{:T(128)}, bf16[3,512,2,256]{3,2,1,0:T(2,128)(2,1)}, f32[3,2,512]{2,1,0:T(2,128)}, bf16[3,512,2,256]{1,3,2,0:T(8,128)(2,1)}, s32[3]{0:T(128)S(...) while((s32[]{:T(128)}, ...), condition=%wide.region_5.6_spmd, body=%wide.region_2.5_spmd.sunk | while | flops 543948288 | bytes 11569293 | solution.py:174
  199.4 1.9 fusion.149
  207.1 1.9 fusion.149
  214.7 1.9 fusion.149
  218.9 2.3 copy.202
  222.3 8.0 fusion.95
  230.4 48.3 %multiply_convert_fusion.1 = (bf16[1536,2048]{1,0:T(8,128)(2,1)S(1)}, f32[1536,2048]{1,0:T(8,128)}, f32[1536,2048]{1,0:T(8,128)}) fusion(f32[2048]{0:T(1024)S(1)} %bitcast.342, bf16[2048,2048]{1,0:T(8,128)(2,1)} %all-gather.11.cloned.1.call-done, bf16[1536,2048]{1,0:T(8,128)(2,1)} %param.21, f32[2048]{0:T(1024)S(1)} %bitcast.338, f32[2048]{0:T(1024)S(1)} %bitcast.316, ...), kind=kOutput, calls=%fused_computation.70 | convolution fusion | flops 13111394304 | bytes 46174208 | tf_op jit(solution)/shard_map/dot_general | solution.py:178
  278.7 2.7 copy-done.52
  281.4 19.6 %fusion.93 = f32[2048,2048]{1,0:T(8,128)} fusion(bf16[1536,2048]{1,0:T(8,128)(2,1)S(1)} %get-tuple-element.368, f32[1536]{0:T(1024)S(1)} %reshape.412, bf16[1536,2048]{1,0:T(8,128)(2,1)} %param.22), kind=kOutput, calls=%fused_computation.220 | convolution fusion | flops 12894339072 | bytes 29366272 | tf_op jit(solution)/shard_map/dot_general | solution.py:60
  302.2 2.9 add_multiply_fusion.3
  305.2 109.2 %reduce-scatter.27.cloned.1.call-done = f32[2048,256]{1,0:T(8,128)} async-done(((f32[2048,2048]{1,0:T(8,128)}), f32[2048,256]{1,0:T(8,128)}) %reduce-scatter.27.cloned.1.call-update) | async-done | bytes 2097168 | tf_op jit(solution)/shard_map/reduce_scatter | solution.py:242
  414.3 6.9 add_multiply_fusion
  421.6 9.6 fusion.86
  432.7 11.6 all-gather.9.cloned.1.call-done
  444.2 8.1 convolution_convert_fusion.1
  452.3 4.0 reshape.405
  456.3 33.5 %while.27 = (s32[]{:T(128)}, f32[3,512,2,256]{1,3,2,0:T(8,128)}, f32[3,512,2,256]{1,3,2,0:T(8,128)}, bf16[3,512,2,256]{1,3,2,0:T(8,128)(2,1)}, bf16[3,512,2,256]...) while((s32[]{:T(128)}, f32[3,512,2,256]{1,3,2,0:T(8,128)}, ...), condition=%wide.region_9.10_spmd, body=%wide.region_7.9_spmd.sunk | while | flops 1347943936 | bytes 36724960 | solution.py:208
  489.8 1.8 slice.142
  491.7 1.8 slice.139
  493.5 1.7 multiply_subtract_fusion.1
  495.5 2.6 convert_reduce_fusion.1
  498.0 11.1 copy.175
  509.1 13.0 %convert_element_type.139 = bf16[1536,1536]{1,0:T(8,128)(2,1)} reshape(bf16[3,512,2,3,256]{4,3,2,1,0:T(4,128)(2,1)} %copy.175) | data formatting | bytes 9437184 | tf_op jit(solution)/shard_map/convert_element_type | solution.py:216
  522.1 26.9 %convert_reduce_fusion = (f32[2048]{0:T(1024)S(1)}, bf16[1536,2048]{1,0:T(8,128)(2,1)}) fusion(f32[1536,2048]{1,0:T(8,128)} %get-tuple-element.369, bf16[2048,2048]{1,0:T(8,128)(2,1)} %all-gather.13.cloned.1.call-done, f32[1536]{0:T(1024)S(1)} %reshape.412, bf16[1536,2048]{1,0:T(8,128)(2,1)} %param.22, f32[1536,2048]{1,0:T(8,128)} %get-tuple-element.429, ...), kind=kOutput, calls=%fused_computation.63 | convolution fusion | flops 12947814400 | bytes 46159872 | tf_op jit(solution)/shard_map/dot_general | solution.py:66
  549.0 19.2 %fusion.109 = f32[1536,2048]{1,0:T(8,128)} fusion(bf16[1536,2048]{1,0:T(8,128)(2,1)} %get-tuple-element.432, bf16[2048,2048]{1,0:T(8,128)(2,1)} %all-gather.11.cloned.1.call-done), kind=kOutput, calls=%fused_computation.229 | convolution fusion | flops 12884901888 | bytes 27262976 | tf_op jit(solution)/shard_map/dot_general | solution.py:66
  568.3 22.1 %fusion.103 = (f32[2048]{0:T(1024)S(1)}, f32[1536]{0:T(1024)S(1)}, f32[1536]{0:T(1024)S(1)}, f32[2048]{0:T(1024)S(1)}, f32[1536,2048]{1,0:T(8,128)}) fusion(f32[2048]{0:T(1024)S(1)} %bitcast.322, f32[1536]{0:T(1024)S(1)} %copy-done.23, bf16[1536,2048]{1,0:T(8,128)(2,1)} %param.21, f32[1536,2048]{1,0:T(8,128)} %fusion.109, f32[2048]{0:T(1024)S(1)} %bitcast.317, ...), kind=kOutput, calls=%fused_computation.224 | convolution fusion | flops 9695125504 | bytes 42518528 | tf_op jit(solution)/shard_map/dot_general | solution.py:66
  590.5 14.1 %multiply_reduce_fusion.1 = (f32[2048]{0:T(1024)S(1)}, f32[1536]{0:T(1024)S(1)}, f32[1536]{0:T(1024)S(1)}, f32[2048]{0:T(1024)S(1)}) fusion(f32[1536,2048]{1,0:T(8,128)} %fusion.109, bf16[1536,2048]{1,0:T(8,128)(2,1)} %param.21, f32[1536]{0:T(1024)S(1)} %copy-done.31, f32[1536]{0:T(1024)S(1)} %copy-done.23, f32[1536]{0:T(1024)S(1)} %get-tuple-element.413, ...), kind=kLoop, calls=%fused_computation.61 | loop fusion | flops 59761664 | bytes 31526912 | tf_op jit(solution)/shard_map/transpose(jvp())/reduce_sum | solution.py:24
  606.6 16.7 %fusion.90 = f32[2048,1536]{1,0:T(8,128)} fusion(bf16[1536,1536]{1,0:T(8,128)(2,1)} %convert_element_type.139, bf16[1536,2048]{1,0:T(8,128)(2,1)} %param.21, f32[2048]{0:T(1024)S(1)} %bitcast.341, f32[2048]{0:T(1024)S(1)} %bitcast.324, f32[1536]{0:T(1024)S(1)} %copy-done.31, f32[1536]{0:T(1024)S(1)} %copy-done.23), kind=kOutput, calls=%fused_computation.217 | convolution fusion | flops 9682550784 | bytes 23621632 | tf_op jit(solution)/shard_map/dot_general | solution.py:60
  624.5 14.5 %reduce-scatter.29.cloned.1.call-done = f32[6,256]{1,0:T(8,128)} async-done(((f32[6,2048]{1,0:T(8,128)}), f32[6,256]{1,0:T(8,128)}) %reduce-scatter.29.cloned.1.call-update) | async-done | bytes 6160 | tf_op jit(solution)/shard_map/reduce_scatter | solution.py:239
  640.5 16.2 %add_convert_fusion = bf16[1536,2048]{1,0:T(8,128)(2,1)} fusion(f32[1536]{0:T(1024)S(1)} %negate_multiply_fusion.1, f32[1536]{0:T(1024)S(1)} %negate_multiply_fusion.2, f32[1536]{0:T(1024)S(1)} %get-tuple-element.412, f32[1536]{0:T(1024)S(1)} %copy-done.23, bf16[1536,2048]{1,0:T(8,128)(2,1)} %param.21, f32[1536]{0:T(1024)S(1)} %copy-done.31, ...), kind=kLoop, calls=%fused_computation.64 | loop fusion | flops 50331648 | bytes 37801984 | tf_op jit(solution)/shard_map/convert_element_type | solution.py:246
  658.1 7.9 fusion.108
  666.0 21.3 %add_convert_fusion.2 = bf16[1536,2048]{1,0:T(8,128)(2,1)} fusion(f32[1536,2048]{1,0:T(8,128)} %fusion.108, bf16[1536,2048]{1,0:T(8,128)(2,1)} %copy-done.52, bf16[2048,2048]{1,0:T(8,128)(2,1)} %all-gather.13.cloned.1.call-done), kind=kOutput, calls=%fused_computation.69 | convolution fusion | flops 12891193344 | bytes 33554432 | tf_op jit(solution)/shard_map/dot_general | solution.py:183
  687.9 24.6 %fusion.88 = f32[2048,2048]{1,0:T(8,128)} fusion(bf16[1536,2048]{1,0:T(8,128)(2,1)} %get-tuple-element.432, bf16[1536,2048]{1,0:T(8,128)(2,1)} %param.21, f32[2048]{0:T(1024)S(1)} %bitcast.339, f32[2048]{0:T(1024)S(1)} %bitcast.320, f32[1536]{0:T(1024)S(1)} %copy-done.31, f32[1536]{0:T(1024)S(1)} %copy-done.23), kind=kOutput, calls=%fused_computation.215 | convolution fusion | flops 12903776256 | bytes 29388800 | tf_op jit(solution)/shard_map/dot_general | solution.py:60
  712.6 9.2 convert_element_type.119
  725.7 47.3 %reduce-scatter.21.cloned.1.call-done = f32[256,1536]{1,0:T(8,128)} async-done(((f32[2048,1536]{1,0:T(8,128)}), f32[256,1536]{1,0:T(8,128)}) %reduce-scatter.21.cloned.1.call-update) | async-done | bytes 1572880 | tf_op jit(solution)/shard_map/reduce_scatter | solution.py:236
  772.9 4.7 add_multiply_fusion.2
  777.6 1.9 pad_maximum_fusion.2
  781.0 2.3 pad_maximum_fusion.1
  783.3 27.3 %reduce-scatter.33.cloned.1.call-done = f32[128,2]{1,0:T(8,128)} async-done(((f32[1024,2]{1,0:T(8,128)}), f32[128,2]{1,0:T(8,128)}) %reduce-scatter.33.cloned.1.call-update) | async-done | bytes 1040
  813.5 19.2 %reduce-scatter.35.cloned.1.call-done = bf16[64,4]{1,0:T(8,128)(2,1)} async-done(((bf16[256,4]{1,0:T(8,128)(2,1)}), bf16[64,4]{1,0:T(8,128)(2,1)}) %reduce-scatter.35.cloned.1.call-update) | async-done | bytes 528
  834.8 109.1 %reduce-scatter.19.cloned.1.call-done = bf16[1536,512]{1,0:T(8,128)(2,1)} async-done(((bf16[1536,2048]{1,0:T(8,128)(2,1)}), bf16[1536,512]{1,0:T(8,128)(2,1)}) %reduce-scatter.19.cloned.1.call-update) | async-done | bytes 1572880 | tf_op jit(solution)/shard_map/reduce_scatter | solution.py:245
  943.8 4.0 add_convert_fusion.5
  947.9 109.6 %reduce-scatter.17.cloned.1.call-done = bf16[1536,512]{1,0:T(8,128)(2,1)} async-done(((bf16[1536,2048]{1,0:T(8,128)(2,1)}), bf16[1536,512]{1,0:T(8,128)(2,1)}) %reduce-scatter.17.cloned.1.call-update) | async-done | bytes 1572880 | tf_op jit(solution)/shard_map/reduce_scatter | solution.py:186
  1057.5 4.0 multiply_convert_fusion.2
  1061.5 116.7 %reduce-scatter.25.cloned.1.call-done = f32[256,2048]{1,0:T(8,128)} async-done(((f32[2048,2048]{1,0:T(8,128)}), f32[256,2048]{1,0:T(8,128)}) %reduce-scatter.25.cloned.1.call-update) | async-done | bytes 2097168 | tf_op jit(solution)/shard_map/reduce_scatter | solution.py:240
  1178.2 5.7 add_multiply_fusion.1
  1183.9 2.5 pad_maximum_fusion
  (260 shorter events, 74.2 us)
Async XLA Ops:
  7.2 5.4 copy-start.46
  7.2 15.7 %copy-start.35 = (f32[6,64]{1,0:T(8,128)S(1)}, f32[6,64]{1,0:T(8,128)}, u32[]{:S(2)}) copy-start(f32[6,64]{1,0:T(8,128)} %param.36) | copy-start | bytes 4612
  7.2 84.9 %copy-start.50 = (s32[3]{0:T(128)S(1)}, s32[3]{0:T(128)}, u32[]{:S(2)}) copy-start(s32[3]{0:T(128)} %param.23) | copy-start | bytes 40
  7.2 85.0 %copy-start.48 = (f32[2,128]{1,0:T(2,128)S(1)}, f32[2,128]{1,0:T(2,128)}, u32[]{:S(2)}) copy-start(f32[2,128]{1,0:T(2,128)} %param.32) | copy-start | bytes 3076
  7.2 104.9 %all-gather.7.cloned.1.call-start = ((), (), s32[]{:S(2)}) async-start(), calls=%async_computation.10 | async-start | bytes 7077888 | tf_op jit(solution)/shard_map/all_gather | solution.py:150
  9.7 220.7 %all-gather.11.cloned.1.call-start = ((), (), s32[]{:S(2)}) async-start(), calls=%async_computation.12 | async-start | bytes 9437184 | tf_op jit(solution)/shard_map/all_gather | solution.py:153
  12.5 288.6 %reduce-scatter.23.cloned.1.call-start = ((), (), s32[]{:S(2)}) async-start(), calls=%async_computation.17 | async-start | bytes 4718592 | tf_op jit(solution)/shard_map/reduce_scatter | solution.py:238
  92.2 429.9 %copy-start.28 = (f32[1536]{0:T(1024)}, f32[1536]{0:T(1024)S(1)}, u32[]{:S(2)}) copy-start(f32[1536]{0:T(1024)S(1)} %reshape.412) | copy-start | bytes 18436
  105.0 125.4 %copy-start.22 = (f32[1536]{0:T(1024)}, f32[1536]{0:T(1024)S(1)}, u32[]{:S(2)}) copy-start(f32[1536]{0:T(1024)S(1)} %broadcast_multiply_fusion) | copy-start | bytes 18436
  109.6 1.8 copy-start.33
  109.6 120.8 %copy-start.30 = (f32[1536]{0:T(1024)}, f32[1536]{0:T(1024)S(1)}, u32[]{:S(2)}) copy-start(f32[1536]{0:T(1024)S(1)} %fusion.64) | copy-start | bytes 18436
  111.4 67.2 %copy-start.9 = (f32[512,32]{1,0:T(8,128)}, f32[512,32]{1,0:T(8,128)S(1)}, u32[]{:S(2)}) copy-start(f32[512,32]{1,0:T(8,128)S(1)} %get-tuple-element.428) | copy-start | bytes 196612
  112.1 16.1 %copy-start.26 = (f32[1,2048]{1,0:T(1,128)}, f32[1,2048]{1,0:T(1,128)S(1)}, u32[]{:S(2)}) copy-start(f32[1,2048]{1,0:T(1,128)S(1)} %get-tuple-element.411) | copy-start | bytes 24580
  112.1 16.1 %copy-start.39 = (f32[1,2048]{1,0:T(1,128)}, f32[1,2048]{1,0:T(1,128)S(1)}, u32[]{:S(2)}) copy-start(f32[1,2048]{1,0:T(1,128)S(1)} %get-tuple-element.410) | copy-start | bytes 24580
  112.1 118.3 %copy-start.24 = (f32[1,2048]{1,0:T(1,128)}, f32[1,2048]{1,0:T(1,128)S(1)}, u32[]{:S(2)}) copy-start(f32[1,2048]{1,0:T(1,128)S(1)} %get-tuple-element.409) | copy-start | bytes 24580
  112.1 118.3 %copy-start.37 = (f32[1,2048]{1,0:T(1,128)}, f32[1,2048]{1,0:T(1,128)S(1)}, u32[]{:S(2)}) copy-start(f32[1,2048]{1,0:T(1,128)S(1)} %get-tuple-element.408) | copy-start | bytes 24580
  151.8 20.1 %copy-start.3 = (bf16[3,512,2,1,256]{4,3,2,1,0:T(2,128)(2,1)}, bf16[3,512,2,1,256]{4,3,2,1,0:T(2,128)(2,1)S(1)}, u32[]{:S(2)}) copy-start(bf16[3,512,2,1,256]{4,3,2,1,0:T(2,128)(2,1)S(1)} %slice.258) | copy-start | bytes 4718596
  175.2 3.4 copy-start.19
  218.9 11.4 copy-start
  230.3 184.0 %reduce-scatter.27.cloned.1.call-start = ((), (), s32[]{:S(2)}) async-start(), calls=%async_computation.19 | async-start | bytes 18874368 | tf_op jit(solution)/shard_map/reduce_scatter | solution.py:242
  278.7 2.7 copy-start.52
  301.0 113.3 %copy-start.11 = (f32[2048,256]{1,0:T(8,128)S(1)}, f32[2048,256]{1,0:T(8,128)}, u32[]{:S(2)}) copy-start(f32[2048,256]{1,0:T(8,128)} %param.34) | copy-start | bytes 6291460
  301.0 143.2 %all-gather.9.cloned.1.call-start = ((), (), s32[]{:S(2)}) async-start(), calls=%async_computation.11 | async-start | bytes 2359296 | tf_op jit(solution)/shard_map/all_gather | solution.py:152
  305.1 116.3 %copy-start.10 = (f32[512,32]{1,0:T(8,128)S(1)}, f32[512,32]{1,0:T(8,128)}, u32[]{:S(2)}) copy-start(f32[512,32]{1,0:T(8,128)} %copy-done.9) | copy-start | bytes 196612
  305.1 116.4 %copy-start.20 = (f32[512,32]{1,0:T(8,128)S(1)}, f32[512,32]{1,0:T(8,128)}, u32[]{:S(2)}) copy-start(f32[512,32]{1,0:T(8,128)} %get-tuple-element.426) | copy-start | bytes 196612
  305.1 217.0 %all-gather.13.cloned.1.call-start = ((), (), s32[]{:S(2)}) async-start(), calls=%async_computation.13 | async-start | bytes 9437184 | tf_op jit(solution)/shard_map/all_gather | solution.py:155
  421.3 217.7 %reduce-scatter.29.cloned.1.call-start = ((), (), s32[]{:S(2)}) async-start(), calls=%async_computation.20 | async-start | bytes 73728 | tf_op jit(solution)/shard_map/reduce_scatter | solution.py:239
  421.6 9.6 copy-start.4
  432.6 23.7 %copy-start.1 = (bf16[3,512,2,256]{3,1,2,0:T(8,128)(2,1)S(1)}, bf16[3,512,2,256]{3,1,2,0:T(8,128)(2,1)}, u32[]{:S(2)}) copy-start(bf16[3,512,2,256]{3,1,2,0:T(8,128)(2,1)} %copy-done) | copy-start | bytes 4718596
  432.6 23.7 %copy-start.2 = (bf16[3,512,2,256]{3,1,2,0:T(8,128)(2,1)S(1)}, bf16[3,512,2,256]{3,1,2,0:T(8,128)(2,1)}, u32[]{:S(2)}) copy-start(bf16[3,512,2,256]{3,1,2,0:T(8,128)(2,1)} %get-tuple-element.625) | copy-start | bytes 4718596
  432.6 23.7 %copy-start.51 = (s32[3]{0:T(128)S(1)}, s32[3]{0:T(128)}, u32[]{:S(2)}) copy-start(s32[3]{0:T(128)} %param.23) | copy-start | bytes 40
  462.3 3.6 copy-start.14
  473.4 3.6 copy-start.14
  484.6 3.6 copy-start.14
  493.5 2.0 copy-start.16
  549.0 19.2 %copy-start.23 = (f32[1536]{0:T(1024)S(1)}, f32[1536]{0:T(1024)}, u32[]{:S(2)}) copy-start(f32[1536]{0:T(1024)} %copy-done.22) | copy-start | bytes 18436
  549.0 19.2 %copy-start.25 = (f32[1,2048]{1,0:T(1,128)S(1)}, f32[1,2048]{1,0:T(1,128)}, u32[]{:S(2)}) copy-start(f32[1,2048]{1,0:T(1,128)} %copy-done.24) | copy-start | bytes 24580
  549.0 19.2 %copy-start.27 = (f32[1,2048]{1,0:T(1,128)S(1)}, f32[1,2048]{1,0:T(1,128)}, u32[]{:S(2)}) copy-start(f32[1,2048]{1,0:T(1,128)} %copy-done.26) | copy-start | bytes 24580
  568.2 22.2 %copy-start.34 = (f32[1536]{0:T(1024)S(1)}, f32[1536]{0:T(1024)}, u32[]{:S(2)}) copy-start(f32[1536]{0:T(1024)} %copy-done.33) | copy-start | bytes 18436
  568.2 22.2 %copy-start.31 = (f32[1536]{0:T(1024)S(1)}, f32[1536]{0:T(1024)}, u32[]{:S(2)}) copy-start(f32[1536]{0:T(1024)} %copy-done.30) | copy-start | bytes 18436
  590.4 14.2 %copy-start.32 = (f32[2048]{0:T(1024)S(1)}, f32[2048]{0:T(1024)}, u32[]{:S(2)}) copy-start(f32[2048]{0:T(1024)} %get-tuple-element.376) | copy-start | bytes 24580
  590.4 16.2 %copy-start.40 = (f32[1,2048]{1,0:T(1,128)S(1)}, f32[1,2048]{1,0:T(1,128)}, u32[]{:S(2)}) copy-start(f32[1,2048]{1,0:T(1,128)} %copy-done.39) | copy-start | bytes 24580
  605.3 118.3 %reduce-scatter.31.cloned.1.call-start = ((), (), s32[]{:S(2)}) async-start(), calls=%async_computation.21 | async-start | bytes 442368
  606.6 166.4 %reduce-scatter.21.cloned.1.call-start = ((), (), s32[]{:S(2)}) async-start(), calls=%async_computation.16 | async-start | bytes 14155776 | tf_op jit(solution)/shard_map/reduce_scatter | solution.py:236
  623.3 187.2 %reduce-scatter.33.cloned.1.call-start = ((), (), s32[]{:S(2)}) async-start(), calls=%async_computation.22 | async-start | bytes 589824
  624.5 208.3 %reduce-scatter.35.cloned.1.call-start = ((), (), s32[]{:S(2)}) async-start(), calls=%async_computation.23 | async-start | bytes 81920
  640.5 303.4 %reduce-scatter.19.cloned.1.call-start = ((), (), s32[]{:S(2)}) async-start(), calls=%async_computation.15 | async-start | bytes 7864320 | tf_op jit(solution)/shard_map/reduce_scatter | solution.py:245
  656.7 400.8 %reduce-scatter.17.cloned.1.call-start = ((), (), s32[]{:S(2)}) async-start(), calls=%async_computation.14 | async-start | bytes 7864320 | tf_op jit(solution)/shard_map/reduce_scatter | solution.py:186
  687.2 490.9 %reduce-scatter.25.cloned.1.call-start = ((), (), s32[]{:S(2)}) async-start(), calls=%async_computation.18 | async-start | bytes 18874368 | tf_op jit(solution)/shard_map/reduce_scatter | solution.py:240
  712.5 10.0 copy-start.41
  712.5 10.0 copy-start.12
  712.6 10.0 copy-start.13
  712.6 11.9 copy-start.44
  712.6 11.9 copy-start.47
  712.6 60.4 %copy-start.8 = (f32[256,1536]{1,0:T(8,128)S(1)}, f32[256,1536]{1,0:T(8,128)}, u32[]{:S(2)}) copy-start(f32[256,1536]{1,0:T(8,128)} %param.24) | copy-start | bytes 4718596
  724.5 53.2 %copy-start.43 = (f32[2,96]{1,0:T(2,128)}, f32[2,96]{1,0:T(2,128)S(1)}, u32[]{:S(2)}) copy-start(f32[2,96]{1,0:T(2,128)S(1)} %copy.188) | copy-start | bytes 2308
  777.6 2.6 copy-start.6
  777.6 3.4 copy-start.7
  779.5 32.0 %copy-start.45 = (f32[2,2,128]{2,1,0:T(2,128)S(1)}, f32[2,2,128]{2,1,0:T(2,128)}, u32[]{:S(2)}) copy-start(f32[2,2,128]{2,1,0:T(2,128)} %param.33) | copy-start | bytes 6148
  779.5 32.0 %copy-start.49 = (f32[2,128]{1,0:T(2,128)S(1)}, f32[2,128]{1,0:T(2,128)}, u32[]{:S(2)}) copy-start(f32[2,128]{1,0:T(2,128)} %param.32) | copy-start | bytes 3076
  779.5 54.7 %copy-start.36 = (f32[6,64]{1,0:T(8,128)S(1)}, f32[6,64]{1,0:T(8,128)}, u32[]{:S(2)}) copy-start(f32[6,64]{1,0:T(8,128)} %param.36) | copy-start | bytes 4612
  783.3 274.2 %copy-start.29 = (f32[1536]{0:T(1024)S(1)}, f32[1536]{0:T(1024)}, u32[]{:S(2)}) copy-start(f32[1536]{0:T(1024)} %copy-done.28) | copy-start | bytes 18436
  811.5 250.0 %copy-start.42 = (f32[2,128]{1,0:T(2,128)}, f32[2,128]{1,0:T(2,128)S(1)}, u32[]{:S(2)}) copy-start(f32[2,128]{1,0:T(2,128)S(1)} %copy.190) | copy-start | bytes 3076
  947.9 230.3 %copy-start.5 = (f32[256,2048]{1,0:T(8,128)S(1)}, f32[256,2048]{1,0:T(8,128)}, u32[]{:S(2)}) copy-start(f32[256,2048]{1,0:T(8,128)} %param.30) | copy-start | bytes 6291460
  (7 other events, 7.9 us)
Sparse Core Ops, SparseCore 0:
  10.5 48.2 all-gather.6
  61.2 54.3 all-gather.10
  230.4 48.3 reduce-scatter.22
  301.1 113.1 reduce-scatter.26
  416.1 28.1 all-gather.8
  446.5 55.8 all-gather.12
  605.5 33.4 reduce-scatter.28
  642.6 33.8 reduce-scatter.30
  680.6 92.2 reduce-scatter.20
  776.4 34.0 reduce-scatter.32
  813.4 19.2 reduce-scatter.34
  834.9 108.9 reduce-scatter.18
  946.1 111.2 reduce-scatter.16
  1061.5 116.6 reduce-scatter.24
where the time goes:
time: 1200 us; the launch traced here: 1190 us
  waiting for transfers between devices  565 us (47%)
  matrix products  267 us (22%)
  other arithmetic  130 us (11%)
  local copies, waits for them, and re-layouts  123 us (10%)
  blocking collectives  88.4 us (7%)
  between operations  14.8 us (1%)
    reduce_scatter x1, waiting for transfers between devices, on_device(): lax.psum_scatter(expand_local, 'dp', scatter_dimension=0, tiled=True)  117 us
    reduce_scatter x1, waiting for transfers between devices, on_device(): lax.psum_scatter(partial_sum.astype(jnp.bfloat16), 'tensor', scatter_dime...  110 us
    reduce_scatter x1, waiting for transfers between devices, on_device(): lax.psum_scatter(shrink_local, 'dp', scatter_dimension=1, tiled=True)  109 us
    reduce_scatter x1, waiting for transfers between devices, on_device(): lax.psum_scatter((dinput_one + dinput_two).astype(jnp.bfloat16), 'tensor'...  109 us
    dot_general x4, matrix products, contract_cols(): lax.dot_general(left, right, (((1,), (1,)), ((), ())), preferred_element_...  76.3 us
    all_gather x1, blocking collectives, on_device(): lax.all_gather(vectors.astype(jnp.bfloat16), ('dp', 'tensor'), axis=1, ti...  69.1 us
    dot_general x4, matrix products, contract_rows(): lax.dot_general(left, right, (((0,), (0,)), ((), ())), preferred_element_...  68.8 us
    dot_general x1, matrix products, on_device(): jnp.dot(normed_two, expand, preferred_element_type=jnp.float32)  48.3 us
  transfers between devices with their start and end apart: 14, of which 9 were waited for; matrix products, arithmetic and copies ran while one was open for 35% of the time, Pallas kernels for 0%

commit v1 on v0

--- a/solution.py
+++ b/solution.py
@@ -15,6 +15,18 @@
 learn_rate = 0.02
 decay_rate = 0.01
 rotary_base = 10000.0
+
+
+def gather_by_bits(value, axis, dim):
+    ways, here = (lax.axis_size(axis), lax.axis_index(axis))
+    grown, reach = (value, 1)
+    while reach < ways:
+        theirs = lax.ppermute(grown, axis, [(d, d ^ reach) for d in range(ways)])
+        mine_first = jnp.concatenate([grown, theirs], axis=dim)
+        theirs_first = jnp.concatenate([theirs, grown], axis=dim)
+        grown = jnp.where(here & reach == 0, mine_first, theirs_first)
+        reach = 2 * reach
+    return grown
 
 
 def norm_layer(values, scale_row, shift_row):
@@ -154,9 +166,9 @@
         lax.all_gather(offsets.astype(jnp.bfloat16), "dp", axis=1, tiled=True),
         lax.all_gather(reducer.astype(jnp.bfloat16), "dp", axis=1, tiled=True),
     )
-    full_vectors = lax.all_gather(
-        vectors.astype(jnp.bfloat16), ("dp", "tensor"), axis=1, tiled=True
-    ).astype(jnp.float32)
+    full_vectors = gather_by_bits(vectors.astype(jnp.bfloat16), ("dp", "tensor"), 1).astype(
+        jnp.float32
+    )
     slot_count = lengths.shape[0]
     row_count = slot_count * SEQ_LEN
     local_heads = entry.shape[1] // (3 * HD)

time: 1200 us -> 1150 us (0.958)
  blocking collectives: 88.4 us -> 18.4 us
  waiting for transfers between devices: 565 us -> 579 us
    all_gather x1 -> x0, blocking collectives: 69.1 us -> none  [on_device(): lax.all_gather(vectors.astype(jnp.bfloat16), ('dp', 'tensor'), axis=1, ti...]
  transfers between devices with their start and end apart: 14 -> 19, of which waited for: 9 -> 12; matrix products, arithmetic and copies ran while one was open for 35% -> 36% of each run, Pallas kernels for 0% -> 0%
where the time goes in v1:
time: 1150 us; the launch traced here: 1140 us
  waiting for transfers between devices  579 us (50%)
  matrix products  266 us (23%)
  other arithmetic  128 us (11%)
  local copies, waits for them, and re-layouts  123 us (11%)
  blocking collectives  18.4 us (2%)
  between operations  14.8 us (1%)
    reduce_scatter x1, waiting for transfers between devices, on_device(): lax.psum_scatter(expand_local, 'dp', scatter_dimension=0, tiled=True)  117 us
    reduce_scatter x1, waiting for transfers between devices, on_device(): lax.psum_scatter(shrink_local, 'dp', scatter_dimension=1, tiled=True)  113 us
    reduce_scatter x1, waiting for transfers between devices, on_device(): lax.psum_scatter(partial_sum.astype(jnp.bfloat16), 'tensor', scatter_dime...  110 us
    reduce_scatter x1, waiting for transfers between devices, on_device(): lax.psum_scatter((dinput_one + dinput_two).astype(jnp.bfloat16), 'tensor'...  109 us
    dot_general x4, matrix products, contract_cols(): lax.dot_general(left, right, (((1,), (1,)), ((), ())), preferred_element_...  76.4 us
    dot_general x4, matrix products, contract_rows(): lax.dot_general(left, right, (((0,), (0,)), ((), ())), preferred_element_...  68.8 us
    dot_general x1, matrix products, on_device(): jnp.dot(normed_two, expand, preferred_element_type=jnp.float32)  47.7 us
    reduce_scatter x1, waiting for transfers between devices, on_device(): lax.psum_scatter(entry_local, 'dp', scatter_dimension=0, tiled=True)  47.3 us
  transfers between devices with their start and end apart: 19, of which 12 were waited for; matrix products, arithmetic and copies ran while one was open for 36% of the time, Pallas kernels for 0%

profile of v1, /device:TPU:0, one launch (start us, length us, event | category | flops | bytes accessed | tf_op | source)
XLA Modules:
  0.0 1142.9 jit_solution(3433127459435759473)
XLA Ops:
  7.2 2.4 convert_element_type.123
  10.4 3.1 collective-permute-start
  13.4 2.7 convert_element_type.128
  16.2 3.8 convert_reduce_fusion.2
  21.2 1.8 multiply_reduce_fusion.5
  24.8 2.5 collective-permute-start.1
  27.4 8.9 all-gather
  36.6 9.6 all_gather.22
  46.9 3.4 collective-permute-done.3
  51.1 3.4 collective-permute-done.4
  55.2 3.8 all-gather.6.cloned.1.call-done
  59.0 15.9 %convolution_add_fusion = f32[1536,1536]{1,0:T(8,128)} fusion(bf16[2048,1536]{1,0:T(8,128)(2,1)} %all-gather.6.cloned.1.call-done, f32[1536]{0:T(1024)S(1)} %reshape.413, bf16[1536,2048]{1,0:T(8,128)(2,1)} %param.21, f32[2048]{0:T(1024)S(1)} %bitcast.332, f32[2048]{0:T(1024)S(1)} %bitcast.313, f32[1536]{0:T(1024)S(1)} %fusion.65, ...), kind=kOutput, calls=%fused_computation.89 | convolution fusion | flops 9684910080 | bytes 22054912 | tf_op jit(solution)/shard_map/dot_general | solution.py:179
  74.9 15.8 %reshape.403 = f32[3,512,2,3,256]{4,3,2,1,0:T(4,128)} reshape(f32[1536,1536]{1,0:T(8,128)} %convolution_add_fusion) | data formatting | bytes 18874368 | tf_op jit(solution)/shard_map/reshape | solution.py:182
  90.7 7.8 slice.258
  98.5 6.6 copy.182
  105.1 13.3 %fusion.106 = (f32[3,512,2,1,256]{4,3,2,1,0:T(1,128)S(1)}, f32[3,512,2,1,256]{4,3,2,1,0:T(1,128)S(1)}) fusion(f32[3,512,2,3,256]{4,3,2,1,0:T(4,128)} %reshape.403), kind=kLoop, calls=%fused_computation.229 | loop fusion | bytes 12582912 | tf_op jit(solution)/shard_map/slice | solution.py:184
  125.1 4.5 subtract_convert_fusion
  129.7 11.1 pad_maximum_fusion.3
  142.4 23.0 %while.26 = (s32[]{:T(128)}, bf16[3,512,2,256]{3,2,1,0:T(2,128)(2,1)}, f32[3,2,512]{2,1,0:T(2,128)}, bf16[3,512,2,256]{1,3,2,0:T(8,128)(2,1)}, s32[3]{0:T(128)S(...) while((s32[]{:T(128)}, ...), condition=%wide.region_5.6_spmd, body=%wide.region_2.5_spmd.sunk | while | flops 543948288 | bytes 11569293 | solution.py:186
  145.9 1.9 fusion.150
  153.6 1.9 fusion.150
  161.2 1.9 fusion.150
  165.4 2.3 copy.198
  168.8 8.0 fusion.96
  176.9 47.7 %multiply_convert_fusion.1 = (bf16[1536,2048]{1,0:T(8,128)(2,1)S(1)}, f32[1536,2048]{1,0:T(8,128)}, f32[1536,2048]{1,0:T(8,128)}) fusion(f32[2048]{0:T(1024)S(1)} %bitcast.334, bf16[2048,2048]{1,0:T(8,128)(2,1)} %all-gather.10.cloned.1.call-done, bf16[1536,2048]{1,0:T(8,128)(2,1)} %param.21, f32[2048]{0:T(1024)S(1)} %bitcast.330, f32[2048]{0:T(1024)S(1)} %bitcast.308, ...), kind=kOutput, calls=%fused_computation.70 | convolution fusion | flops 13111394304 | bytes 46174208 | tf_op jit(solution)/shard_map/dot_general | solution.py:190
  224.7 2.7 copy-done.52
  227.4 19.6 %fusion.94 = f32[2048,2048]{1,0:T(8,128)} fusion(bf16[1536,2048]{1,0:T(8,128)(2,1)S(1)} %get-tuple-element.368, f32[1536]{0:T(1024)S(1)} %reshape.412, bf16[1536,2048]{1,0:T(8,128)(2,1)} %param.22), kind=kOutput, calls=%fused_computation.224 | convolution fusion | flops 12894339072 | bytes 29366272 | tf_op jit(solution)/shard_map/dot_general | solution.py:72
  248.2 2.9 add_multiply_fusion.3
  251.1 112.8 %reduce-scatter.27.cloned.1.call-done = f32[2048,256]{1,0:T(8,128)} async-done(((f32[2048,2048]{1,0:T(8,128)}), f32[2048,256]{1,0:T(8,128)}) %reduce-scatter.27.cloned.1.call-update) | async-done | bytes 2097168 | tf_op jit(solution)/shard_map/reduce_scatter | solution.py:254
  363.9 6.9 add_multiply_fusion
  371.1 9.6 fusion.87
  382.2 11.5 %all-gather.8.cloned.1.call-done = bf16[512,2048]{1,0:T(8,128)(2,1)} async-done(((bf16[512,256]{1,0:T(8,128)(2,1)}), bf16[512,2048]{1,0:T(8,128)(2,1)}) %all-gather.8.cloned.1.call-update) | async-done | bytes 2097168 | tf_op jit(solution)/shard_map/all_gather | solution.py:164
  393.8 8.1 convolution_convert_fusion.1
  401.9 4.0 reshape.405
  405.9 33.5 %while.27 = (s32[]{:T(128)}, f32[3,512,2,256]{1,3,2,0:T(8,128)}, f32[3,512,2,256]{1,3,2,0:T(8,128)}, bf16[3,512,2,256]{1,3,2,0:T(8,128)(2,1)}, bf16[3,512,2,256]...) while((s32[]{:T(128)}, f32[3,512,2,256]{1,3,2,0:T(8,128)}, ...), condition=%wide.region_9.10_spmd, body=%wide.region_7.9_spmd.sunk | while | flops 1347943936 | bytes 36724960 | solution.py:220
  439.4 1.8 slice.142
  441.2 1.8 slice.139
  445.0 2.6 convert_reduce_fusion.1
  447.6 11.1 copy.171
  458.7 13.0 %convert_element_type.139 = bf16[1536,1536]{1,0:T(8,128)(2,1)} reshape(bf16[3,512,2,3,256]{4,3,2,1,0:T(4,128)(2,1)} %copy.171) | data formatting | bytes 9437184 | tf_op jit(solution)/shard_map/convert_element_type | solution.py:228
  471.7 26.9 %convert_reduce_fusion = (f32[2048]{0:T(1024)S(1)}, bf16[1536,2048]{1,0:T(8,128)(2,1)}) fusion(f32[1536,2048]{1,0:T(8,128)} %get-tuple-element.369, bf16[2048,2048]{1,0:T(8,128)(2,1)} %all-gather.12.cloned.1.call-done, f32[1536]{0:T(1024)S(1)} %reshape.412, bf16[1536,2048]{1,0:T(8,128)(2,1)} %param.22, f32[1536,2048]{1,0:T(8,128)} %get-tuple-element.429, ...), kind=kOutput, calls=%fused_computation.63 | convolution fusion | flops 12947814400 | bytes 46159872 | tf_op jit(solution)/shard_map/dot_general | solution.py:78
  498.6 19.2 %fusion.110 = f32[1536,2048]{1,0:T(8,128)} fusion(bf16[1536,2048]{1,0:T(8,128)(2,1)} %get-tuple-element.432, bf16[2048,2048]{1,0:T(8,128)(2,1)} %all-gather.10.cloned.1.call-done), kind=kOutput, calls=%fused_computation.233 | convolution fusion | flops 12884901888 | bytes 27262976 | tf_op jit(solution)/shard_map/dot_general | solution.py:78
  517.8 22.2 %fusion.104 = (f32[2048]{0:T(1024)S(1)}, f32[1536]{0:T(1024)S(1)}, f32[1536]{0:T(1024)S(1)}, f32[2048]{0:T(1024)S(1)}, f32[1536,2048]{1,0:T(8,128)}) fusion(f32[2048]{0:T(1024)S(1)} %bitcast.314, f32[1536]{0:T(1024)S(1)} %copy-done.24, bf16[1536,2048]{1,0:T(8,128)(2,1)} %param.21, f32[1536,2048]{1,0:T(8,128)} %fusion.110, f32[2048]{0:T(1024)S(1)} %bitcast.309, ...), kind=kOutput, calls=%fused_computation.228 | convolution fusion | flops 9695125504 | bytes 42518528 | tf_op jit(solution)/shard_map/dot_general | solution.py:78
  540.1 14.1 %multiply_reduce_fusion.1 = (f32[2048]{0:T(1024)S(1)}, f32[1536]{0:T(1024)S(1)}, f32[1536]{0:T(1024)S(1)}, f32[2048]{0:T(1024)S(1)}) fusion(f32[1536,2048]{1,0:T(8,128)} %fusion.110, bf16[1536,2048]{1,0:T(8,128)(2,1)} %param.21, f32[1536]{0:T(1024)S(1)} %copy-done.32, f32[1536]{0:T(1024)S(1)} %copy-done.24, f32[1536]{0:T(1024)S(1)} %get-tuple-element.413, ...), kind=kLoop, calls=%fused_computation.61 | loop fusion | flops 59761664 | bytes 31526912 | tf_op jit(solution)/shard_map/transpose(jvp())/reduce_sum | solution.py:36
  556.2 16.7 %fusion.91 = f32[2048,1536]{1,0:T(8,128)} fusion(bf16[1536,1536]{1,0:T(8,128)(2,1)} %convert_element_type.139, bf16[1536,2048]{1,0:T(8,128)(2,1)} %param.21, f32[2048]{0:T(1024)S(1)} %bitcast.333, f32[2048]{0:T(1024)S(1)} %bitcast.316, f32[1536]{0:T(1024)S(1)} %copy-done.32, f32[1536]{0:T(1024)S(1)} %copy-done.24), kind=kOutput, calls=%fused_computation.221 | convolution fusion | flops 9682550784 | bytes 23621632 | tf_op jit(solution)/shard_map/dot_general | solution.py:72
  574.1 14.5 %reduce-scatter.29.cloned.1.call-done = f32[6,256]{1,0:T(8,128)} async-done(((f32[6,2048]{1,0:T(8,128)}), f32[6,256]{1,0:T(8,128)}) %reduce-scatter.29.cloned.1.call-update) | async-done | bytes 6160 | tf_op jit(solution)/shard_map/reduce_scatter | solution.py:251
  590.2 16.2 %add_convert_fusion = bf16[1536,2048]{1,0:T(8,128)(2,1)} fusion(f32[1536]{0:T(1024)S(1)} %negate_multiply_fusion.1, f32[1536]{0:T(1024)S(1)} %negate_multiply_fusion.2, f32[1536]{0:T(1024)S(1)} %get-tuple-element.412, f32[1536]{0:T(1024)S(1)} %copy-done.24, bf16[1536,2048]{1,0:T(8,128)(2,1)} %param.21, f32[1536]{0:T(1024)S(1)} %copy-done.32, ...), kind=kLoop, calls=%fused_computation.64 | loop fusion | flops 50331648 | bytes 37801984 | tf_op jit(solution)/shard_map/convert_element_type | solution.py:258
  607.7 7.8 fusion.109
  615.6 21.3 %add_convert_fusion.2 = bf16[1536,2048]{1,0:T(8,128)(2,1)} fusion(f32[1536,2048]{1,0:T(8,128)} %fusion.109, bf16[1536,2048]{1,0:T(8,128)(2,1)} %copy-done.52, bf16[2048,2048]{1,0:T(8,128)(2,1)} %all-gather.12.cloned.1.call-done), kind=kOutput, calls=%fused_computation.69 | convolution fusion | flops 12891193344 | bytes 33554432 | tf_op jit(solution)/shard_map/dot_general | solution.py:195
  637.5 24.6 %fusion.89 = f32[2048,2048]{1,0:T(8,128)} fusion(bf16[1536,2048]{1,0:T(8,128)(2,1)} %get-tuple-element.432, bf16[1536,2048]{1,0:T(8,128)(2,1)} %param.21, f32[2048]{0:T(1024)S(1)} %bitcast.331, f32[2048]{0:T(1024)S(1)} %bitcast.312, f32[1536]{0:T(1024)S(1)} %copy-done.32, f32[1536]{0:T(1024)S(1)} %copy-done.24), kind=kOutput, calls=%fused_computation.219 | convolution fusion | flops 12903776256 | bytes 29388800 | tf_op jit(solution)/shard_map/dot_general | solution.py:72
  662.2 9.2 convert_element_type.119
  675.3 47.3 %reduce-scatter.21.cloned.1.call-done = f32[256,1536]{1,0:T(8,128)} async-done(((f32[2048,1536]{1,0:T(8,128)}), f32[256,1536]{1,0:T(8,128)}) %reduce-scatter.21.cloned.1.call-update) | async-done | bytes 1572880 | tf_op jit(solution)/shard_map/reduce_scatter | solution.py:248
  722.6 4.7 add_multiply_fusion.2
  727.3 1.9 pad_maximum_fusion.2
  730.6 2.3 pad_maximum_fusion.1
  732.9 27.3 %reduce-scatter.33.cloned.1.call-done = f32[128,2]{1,0:T(8,128)} async-done(((f32[1024,2]{1,0:T(8,128)}), f32[128,2]{1,0:T(8,128)}) %reduce-scatter.33.cloned.1.call-update) | async-done | bytes 1040
  763.2 19.2 %reduce-scatter.35.cloned.1.call-done = bf16[64,4]{1,0:T(8,128)(2,1)} async-done(((bf16[256,4]{1,0:T(8,128)(2,1)}), bf16[64,4]{1,0:T(8,128)(2,1)}) %reduce-scatter.35.cloned.1.call-update) | async-done | bytes 528
  784.5 109.1 %reduce-scatter.19.cloned.1.call-done = bf16[1536,512]{1,0:T(8,128)(2,1)} async-done(((bf16[1536,2048]{1,0:T(8,128)(2,1)}), bf16[1536,512]{1,0:T(8,128)(2,1)}) %reduce-scatter.19.cloned.1.call-update) | async-done | bytes 1572880 | tf_op jit(solution)/shard_map/reduce_scatter | solution.py:257
  893.6 4.0 add_convert_fusion.5
  897.6 109.6 %reduce-scatter.17.cloned.1.call-done = bf16[1536,512]{1,0:T(8,128)(2,1)} async-done(((bf16[1536,2048]{1,0:T(8,128)(2,1)}), bf16[1536,512]{1,0:T(8,128)(2,1)}) %reduce-scatter.17.cloned.1.call-update) | async-done | bytes 1572880 | tf_op jit(solution)/shard_map/reduce_scatter | solution.py:198
  1007.2 4.0 multiply_convert_fusion.2
  1011.2 116.7 %reduce-scatter.25.cloned.1.call-done = f32[256,2048]{1,0:T(8,128)} async-done(((f32[2048,2048]{1,0:T(8,128)}), f32[256,2048]{1,0:T(8,128)}) %reduce-scatter.25.cloned.1.call-update) | async-done | bytes 2097168 | tf_op jit(solution)/shard_map/reduce_scatter | solution.py:252
  1127.9 5.7 add_multiply_fusion.1
  1133.7 2.5 pad_maximum_fusion
  (272 shorter events, 84.5 us)
Async XLA Ops:
  7.2 51.8 %all-gather.6.cloned.1.call-start = ((), (), s32[]{:S(2)}) async-start(), calls=%async_computation.10 | async-start | bytes 7077888 | tf_op jit(solution)/shard_map/all_gather | solution.py:162
  9.6 167.3 %all-gather.10.cloned.1.call-start = ((), (), s32[]{:S(2)}) async-start(), calls=%async_computation.12 | async-start | bytes 9437184 | tf_op jit(solution)/shard_map/all_gather | solution.py:165
  10.4 14.4 %collective-permute-start = (bf16[6,64]{1,0:T(8,128)(2,1)S(1)}, bf16[6,64]{1,0:T(8,128)(2,1)S(1)}, u32[]{:S(2)}, u32[]{:S(2)}) collective-permute-start(bf16[6,64]{1,0:T(8,128)(2,1)S(1)} %convert_element_type.120), channel_id=1, source_target_pairs={{0,1},{1,0},{2,3},{3,2},{4,5},{5,4},{6,7},{7,6},{8,9},{9,8},{10,11... | collective-permute-start | bytes 2312 | tf_op jit(solution)/shard_map/ppermute | solution.py:24
  16.2 230.9 %reduce-scatter.23.cloned.1.call-start = ((), (), s32[]{:S(2)}) async-start(), calls=%async_computation.17 | async-start | bytes 4718592 | tf_op jit(solution)/shard_map/reduce_scatter | solution.py:250
  16.2 5.0 copy-start
  20.1 7.3 copy-start.46
  20.1 16.6 %copy-start.48 = (f32[2,128]{1,0:T(2,128)S(1)}, f32[2,128]{1,0:T(2,128)}, u32[]{:S(2)}) copy-start(f32[2,128]{1,0:T(2,128)} %param.32) | copy-start | bytes 3076
  20.1 30.9 %copy-start.50 = (s32[3]{0:T(128)S(1)}, s32[3]{0:T(128)}, u32[]{:S(2)}) copy-start(s32[3]{0:T(128)} %param.23) | copy-start | bytes 40
  21.2 155.7 %copy-start.23 = (f32[1536]{0:T(1024)}, f32[1536]{0:T(1024)S(1)}, u32[]{:S(2)}) copy-start(f32[1536]{0:T(1024)S(1)} %broadcast_multiply_fusion) | copy-start | bytes 18436
  23.0 31.6 %copy-start.34 = (f32[1536]{0:T(1024)}, f32[1536]{0:T(1024)S(1)}, u32[]{:S(2)}) copy-start(f32[1536]{0:T(1024)S(1)} %multiply_reduce_fusion.5) | copy-start | bytes 18436
  23.0 153.9 %copy-start.31 = (f32[1536]{0:T(1024)}, f32[1536]{0:T(1024)S(1)}, u32[]{:S(2)}) copy-start(f32[1536]{0:T(1024)S(1)} %fusion.65) | copy-start | bytes 18436
  24.8 100.4 %copy-start.10 = (f32[512,32]{1,0:T(8,128)}, f32[512,32]{1,0:T(8,128)S(1)}, u32[]{:S(2)}) copy-start(f32[512,32]{1,0:T(8,128)S(1)} %get-tuple-element.428) | copy-start | bytes 196612
  24.8 11.4 collective-permute-start.1
  36.2 10.0 collective-permute-start.2
  46.2 4.0 collective-permute-start.3
  50.3 4.3 collective-permute-start.4
  51.1 420.6 %copy-start.29 = (f32[1536]{0:T(1024)}, f32[1536]{0:T(1024)S(1)}, u32[]{:S(2)}) copy-start(f32[1536]{0:T(1024)S(1)} %reshape.412) | copy-start | bytes 18436
  55.2 19.7 %copy-start.27 = (f32[1,2048]{1,0:T(1,128)}, f32[1,2048]{1,0:T(1,128)S(1)}, u32[]{:S(2)}) copy-start(f32[1,2048]{1,0:T(1,128)S(1)} %get-tuple-element.411) | copy-start | bytes 24580
  55.2 19.7 %copy-start.39 = (f32[1,2048]{1,0:T(1,128)}, f32[1,2048]{1,0:T(1,128)S(1)}, u32[]{:S(2)}) copy-start(f32[1,2048]{1,0:T(1,128)S(1)} %get-tuple-element.410) | copy-start | bytes 24580
  55.2 121.7 %copy-start.25 = (f32[1,2048]{1,0:T(1,128)}, f32[1,2048]{1,0:T(1,128)S(1)}, u32[]{:S(2)}) copy-start(f32[1,2048]{1,0:T(1,128)S(1)} %get-tuple-element.409) | copy-start | bytes 24580
  55.2 121.7 %copy-start.37 = (f32[1,2048]{1,0:T(1,128)}, f32[1,2048]{1,0:T(1,128)S(1)}, u32[]{:S(2)}) copy-start(f32[1,2048]{1,0:T(1,128)S(1)} %get-tuple-element.408) | copy-start | bytes 24580
  98.5 19.9 %copy-start.4 = (bf16[3,512,2,1,256]{4,3,2,1,0:T(2,128)(2,1)}, bf16[3,512,2,1,256]{4,3,2,1,0:T(2,128)(2,1)S(1)}, u32[]{:S(2)}) copy-start(bf16[3,512,2,1,256]{4,3,2,1,0:T(2,128)(2,1)S(1)} %slice.258) | copy-start | bytes 4718596
  165.4 11.4 copy-start.1
  176.8 187.1 %reduce-scatter.27.cloned.1.call-start = ((), (), s32[]{:S(2)}) async-start(), calls=%async_computation.19 | async-start | bytes 18874368 | tf_op jit(solution)/shard_map/reduce_scatter | solution.py:254
  247.0 116.9 %copy-start.12 = (f32[2048,256]{1,0:T(8,128)S(1)}, f32[2048,256]{1,0:T(8,128)}, u32[]{:S(2)}) copy-start(f32[2048,256]{1,0:T(8,128)} %param.34) | copy-start | bytes 6291460
  247.0 146.8 %all-gather.8.cloned.1.call-start = ((), (), s32[]{:S(2)}) async-start(), calls=%async_computation.11 | async-start | bytes 2359296 | tf_op jit(solution)/shard_map/all_gather | solution.py:164
  251.0 119.9 %copy-start.11 = (f32[512,32]{1,0:T(8,128)S(1)}, f32[512,32]{1,0:T(8,128)}, u32[]{:S(2)}) copy-start(f32[512,32]{1,0:T(8,128)} %copy-done.10) | copy-start | bytes 196612
  251.1 120.0 %copy-start.21 = (f32[512,32]{1,0:T(8,128)S(1)}, f32[512,32]{1,0:T(8,128)}, u32[]{:S(2)}) copy-start(f32[512,32]{1,0:T(8,128)} %get-tuple-element.426) | copy-start | bytes 196612
  251.1 220.7 %all-gather.12.cloned.1.call-start = ((), (), s32[]{:S(2)}) async-start(), calls=%async_computation.13 | async-start | bytes 9437184 | tf_op jit(solution)/shard_map/all_gather | solution.py:167
  370.8 217.8 %reduce-scatter.29.cloned.1.call-start = ((), (), s32[]{:S(2)}) async-start(), calls=%async_computation.20 | async-start | bytes 73728 | tf_op jit(solution)/shard_map/reduce_scatter | solution.py:251
  371.1 9.6 copy-start.5
  382.2 23.7 %copy-start.2 = (bf16[3,512,2,256]{3,1,2,0:T(8,128)(2,1)S(1)}, bf16[3,512,2,256]{3,1,2,0:T(8,128)(2,1)}, u32[]{:S(2)}) copy-start(bf16[3,512,2,256]{3,1,2,0:T(8,128)(2,1)} %copy-done.1) | copy-start | bytes 4718596
  382.2 23.7 %copy-start.3 = (bf16[3,512,2,256]{3,1,2,0:T(8,128)(2,1)S(1)}, bf16[3,512,2,256]{3,1,2,0:T(8,128)(2,1)}, u32[]{:S(2)}) copy-start(bf16[3,512,2,256]{3,1,2,0:T(8,128)(2,1)} %get-tuple-element.625) | copy-start | bytes 4718596
  382.2 23.7 %copy-start.51 = (s32[3]{0:T(128)S(1)}, s32[3]{0:T(128)}, u32[]{:S(2)}) copy-start(s32[3]{0:T(128)} %param.23) | copy-start | bytes 40
  411.8 3.6 copy-start.15
  423.0 3.6 copy-start.15
  434.1 3.6 copy-start.15
  498.6 19.2 %copy-start.24 = (f32[1536]{0:T(1024)S(1)}, f32[1536]{0:T(1024)}, u32[]{:S(2)}) copy-start(f32[1536]{0:T(1024)} %copy-done.23) | copy-start | bytes 18436
  498.6 19.2 %copy-start.26 = (f32[1,2048]{1,0:T(1,128)S(1)}, f32[1,2048]{1,0:T(1,128)}, u32[]{:S(2)}) copy-start(f32[1,2048]{1,0:T(1,128)} %copy-done.25) | copy-start | bytes 24580
  498.6 19.2 %copy-start.28 = (f32[1,2048]{1,0:T(1,128)S(1)}, f32[1,2048]{1,0:T(1,128)}, u32[]{:S(2)}) copy-start(f32[1,2048]{1,0:T(1,128)} %copy-done.27) | copy-start | bytes 24580
  517.8 22.2 %copy-start.35 = (f32[1536]{0:T(1024)S(1)}, f32[1536]{0:T(1024)}, u32[]{:S(2)}) copy-start(f32[1536]{0:T(1024)} %copy-done.34) | copy-start | bytes 18436
  517.8 22.2 %copy-start.32 = (f32[1536]{0:T(1024)S(1)}, f32[1536]{0:T(1024)}, u32[]{:S(2)}) copy-start(f32[1536]{0:T(1024)} %copy-done.31) | copy-start | bytes 18436
  540.0 14.2 %copy-start.33 = (f32[2048]{0:T(1024)S(1)}, f32[2048]{0:T(1024)}, u32[]{:S(2)}) copy-start(f32[2048]{0:T(1024)} %get-tuple-element.376) | copy-start | bytes 24580
  540.1 16.2 %copy-start.40 = (f32[1,2048]{1,0:T(1,128)S(1)}, f32[1,2048]{1,0:T(1,128)}, u32[]{:S(2)}) copy-start(f32[1,2048]{1,0:T(1,128)} %copy-done.39) | copy-start | bytes 24580
  555.0 118.2 %reduce-scatter.31.cloned.1.call-start = ((), (), s32[]{:S(2)}) async-start(), calls=%async_computation.21 | async-start | bytes 442368
  556.2 166.4 %reduce-scatter.21.cloned.1.call-start = ((), (), s32[]{:S(2)}) async-start(), calls=%async_computation.16 | async-start | bytes 14155776 | tf_op jit(solution)/shard_map/reduce_scatter | solution.py:248
  572.9 187.3 %reduce-scatter.33.cloned.1.call-start = ((), (), s32[]{:S(2)}) async-start(), calls=%async_computation.22 | async-start | bytes 589824
  574.1 208.3 %reduce-scatter.35.cloned.1.call-start = ((), (), s32[]{:S(2)}) async-start(), calls=%async_computation.23 | async-start | bytes 81920
  590.1 303.5 %reduce-scatter.19.cloned.1.call-start = ((), (), s32[]{:S(2)}) async-start(), calls=%async_computation.15 | async-start | bytes 7864320 | tf_op jit(solution)/shard_map/reduce_scatter | solution.py:257
  606.4 400.8 %reduce-scatter.17.cloned.1.call-start = ((), (), s32[]{:S(2)}) async-start(), calls=%async_computation.14 | async-start | bytes 7864320 | tf_op jit(solution)/shard_map/reduce_scatter | solution.py:198
  636.9 491.1 %reduce-scatter.25.cloned.1.call-start = ((), (), s32[]{:S(2)}) async-start(), calls=%async_computation.18 | async-start | bytes 18874368 | tf_op jit(solution)/shard_map/reduce_scatter | solution.py:252
  662.1 9.3 copy-start.41
  662.2 10.0 copy-start.13
  662.2 10.0 copy-start.14
  662.2 11.9 %copy-start.44 = (f32[2,2,96]{2,1,0:T(2,128)S(1)}, f32[2,2,96]{2,1,0:T(2,128)}, u32[]{:S(2)}) copy-start(f32[2,2,96]{2,1,0:T(2,128)} %param.27) | copy-start | bytes 4612
  662.2 11.9 %copy-start.47 = (f32[2,96]{1,0:T(2,128)S(1)}, f32[2,96]{1,0:T(2,128)}, u32[]{:S(2)}) copy-start(f32[2,96]{1,0:T(2,128)} %param.26) | copy-start | bytes 2308
  662.2 60.4 %copy-start.9 = (f32[256,1536]{1,0:T(8,128)S(1)}, f32[256,1536]{1,0:T(8,128)}, u32[]{:S(2)}) copy-start(f32[256,1536]{1,0:T(8,128)} %param.24) | copy-start | bytes 4718596
  674.1 53.2 %copy-start.43 = (f32[2,96]{1,0:T(2,128)}, f32[2,96]{1,0:T(2,128)S(1)}, u32[]{:S(2)}) copy-start(f32[2,96]{1,0:T(2,128)S(1)} %copy.184) | copy-start | bytes 2308
  729.1 32.0 %copy-start.45 = (f32[2,2,128]{2,1,0:T(2,128)S(1)}, f32[2,2,128]{2,1,0:T(2,128)}, u32[]{:S(2)}) copy-start(f32[2,2,128]{2,1,0:T(2,128)} %param.33) | copy-start | bytes 6148
  729.2 32.0 %copy-start.49 = (f32[2,128]{1,0:T(2,128)S(1)}, f32[2,128]{1,0:T(2,128)}, u32[]{:S(2)}) copy-start(f32[2,128]{1,0:T(2,128)} %param.32) | copy-start | bytes 3076
  729.2 54.7 %copy-start.36 = (f32[6,64]{1,0:T(8,128)S(1)}, f32[6,64]{1,0:T(8,128)}, u32[]{:S(2)}) copy-start(f32[6,64]{1,0:T(8,128)} %param.36) | copy-start | bytes 4612
  732.9 274.3 %copy-start.30 = (f32[1536]{0:T(1024)S(1)}, f32[1536]{0:T(1024)}, u32[]{:S(2)}) copy-start(f32[1536]{0:T(1024)} %copy-done.29) | copy-start | bytes 18436
  761.2 250.0 %copy-start.42 = (f32[2,128]{1,0:T(2,128)}, f32[2,128]{1,0:T(2,128)S(1)}, u32[]{:S(2)}) copy-start(f32[2,128]{1,0:T(2,128)S(1)} %copy.186) | copy-start | bytes 3076
  897.6 230.3 %copy-start.6 = (f32[256,2048]{1,0:T(8,128)S(1)}, f32[256,2048]{1,0:T(8,128)}, u32[]{:S(2)}) copy-start(f32[256,2048]{1,0:T(8,128)} %param.30) | copy-start | bytes 6291460
  (12 other events, 21.9 us)
Sparse Core Ops, SparseCore 0:
  10.5 48.4 all-gather.5
  61.4 54.2 all-gather.9
  176.9 51.7 reduce-scatter.22
  247.1 116.7 reduce-scatter.26
  365.6 28.1 all-gather.7
  396.1 55.8 all-gather.11
  555.1 33.5 reduce-scatter.28
  592.3 33.8 reduce-scatter.30
  630.3 92.2 reduce-scatter.20
  726.1 34.1 reduce-scatter.32
  763.1 19.2 reduce-scatter.34
  784.6 108.9 reduce-scatter.18
  895.9 111.2 reduce-scatter.16
  1011.2 116.6 reduce-scatter.24
